TPU v7x, 32 devices: a whole 2x2x4 slice. The times are simulated.
32 devices in a mesh: slab: 4 (over y, core), pencil: 8 (over z, x).
Axes of the slice: x: 2, y: 2, z: 4, core: 2. Of those that a mesh axis runs over, the one named last changes fastest.
Arguments:
- density: float32 [128, 768, 512], P('pencil', None, 'slab'), may hold values from -6 to 6
- source: float32 [128, 768, 512], P('pencil', None, 'slab'), may hold values from -6 to 8
- coupling: float32 [3], replicated, may hold values from 0.25 to 2, as said below
- width_inverse: float32 [6, 128, 128], replicated, as said below
- height_inverse: float32 [1, 128, 128], replicated, as said below
- depth_inverse: float32 [4, 128, 128], replicated, as said below
Outputs:
- stepped: float32 [128, 768, 512], P('pencil', None, 'slab')
Inputs may be any that keep to these rules, and one draw needn't show every extreme that they name: coupling holds three positive coefficients. `width_inverse`: block i is the inverse of the i-th pivot block of the block LU factorization of the tridiagonal line matrix with diagonal 1 + 2 s and off-diagonals -s, s the matching coupling. `height_inverse`: as for width_inverse, for the height lines. `depth_inverse`: as for width_inverse, for the depth lines.
All inputs are finite; a program needn't handle non-finite values.
Results may differ from a plain program's by a relative error of at most 0.00027.
Values sent between devices are 32-bit elements; how exact they have to be, the bound alone decides.
A program may use at most 128 MiB of HBM per device.

v0:
```python
import jax
import jax.numpy as jnp
from jax import lax
from jax.sharding import PartitionSpec as P


def extended(value, sides, width):
    for axis, dim in sides:
        count, length = (lax.axis_size(axis), value.shape[dim])
        up = [(i, (i + 1) % count) for i in range(count - 1)]
        down = [(j, i) for i, j in up]
        last = lax.slice_in_dim(value, length - width, length, axis=dim)
        leading = lax.slice_in_dim(value, 0, width, axis=dim)
        before = lax.ppermute(last, axis, up)
        after = lax.ppermute(leading, axis, down)
        value = jnp.concatenate([before, value, after], axis=dim)
    return value


def entering(part, axis, combine, identity, reverse):
    count = lax.axis_size(axis)
    place = lax.axis_index(axis)
    ahead = count - 1 - place if reverse else place
    gathered = jax.tree.map(lambda a: lax.all_gather(a, axis), part)
    state = jax.tree.map(lambda a, e: jnp.zeros_like(a) + jnp.asarray(e, a.dtype), part, identity)

    def one(step, state):
        source = count - 1 - step if reverse else step
        return combine(
            state, jax.tree.map(lambda a: lax.dynamic_index_in_dim(a, source, 0, False), gathered)
        )

    return lax.fori_loop(0, ahead, one, state)


def solve_inner(rhs, inverses, strength):
    outer, length, inner = rhs.shape
    size = inverses.shape[1]
    count = length // size
    blocked = rhs.reshape(outer, count, size, inner)

    def forward(current, state):
        result, carry = state
        piece = lax.dynamic_index_in_dim(blocked, current, 1, keepdims=False)
        matrix = lax.dynamic_index_in_dim(inverses, current, 0, keepdims=False)
        value = jnp.einsum("pkq,jk->pjq", piece, matrix, precision=lax.Precision.HIGHEST)
        value = value + strength * matrix[:, 0][None, :, None] * carry[:, None, :]
        result = lax.dynamic_update_index_in_dim(result, value, current, 1)
        return (result, value[:, size - 1, :])

    start = (jnp.zeros_like(blocked), jnp.zeros((outer, inner), blocked.dtype))
    halfway, unused = lax.fori_loop(0, count, forward, start)

    def backward(step, state):
        result, carry = state
        current = count - 1 - step
        value = lax.dynamic_index_in_dim(result, current, 1, keepdims=False)
        matrix = lax.dynamic_index_in_dim(inverses, current, 0, keepdims=False)
        value = value + strength * matrix[:, size - 1][None, :, None] * carry[:, None, :]
        result = lax.dynamic_update_index_in_dim(result, value, current, 1)
        return (result, value[:, 0, :])

    final, unused = lax.fori_loop(
        0, count, backward, (halfway, jnp.zeros((outer, inner), blocked.dtype))
    )
    return final.reshape(outer, length, inner)


def affine_combine(earlier, later):
    return (later[0] * earlier[0], later[0] * earlier[1] + later[1])


def per_device(density, source, coupling, width_inverse, height_inverse, depth_inverse):
    padded = extended(density, (("slab", 2), ("pencil", 0)), 1)
    center = padded[1:-1, :, 1:-1]
    along_height = padded[2:, :, 1:-1] + padded[:-2, :, 1:-1] - 2.0 * center
    along_depth = padded[1:-1, :, 2:] + padded[1:-1, :, :-2] - 2.0 * center
    width_padded = jnp.pad(density, ((0, 0), (1, 1), (0, 0)))
    along_width = width_padded[:, 2:, :] + width_padded[:, :-2, :] - 2.0 * density
    explicit = (
        2.0 * (coupling[0] * along_width + coupling[1] * along_height + coupling[2] * along_depth)
        + source
    )
    width_step = solve_inner(explicit, width_inverse, coupling[0])
    piece = lax.all_to_all(width_step, "pencil", split_axis=1, concat_axis=0, tiled=True)
    height_step = solve_inner(
        piece.reshape(1, piece.shape[0], -1), height_inverse, coupling[1]
    ).reshape(piece.shape)
    size = depth_inverse.shape[1]
    strength = coupling[2]
    matrix = lax.dynamic_index_in_dim(depth_inverse, lax.axis_index("slab"), 0, keepdims=False)
    local_value = jnp.einsum("yxk,jk->yxj", height_step, matrix, precision=lax.Precision.HIGHEST)
    forward_factor = jnp.reshape(strength * matrix[size - 1, 0], (1, 1))
    unit = jnp.ones((1, 1), local_value.dtype)
    zero_rows = jnp.zeros(local_value.shape[:2], local_value.dtype)
    unused, carry_in = entering(
        (forward_factor, local_value[:, :, size - 1]),
        "slab",
        affine_combine,
        (unit, zero_rows),
        False,
    )
    forward_value = local_value + strength * matrix[:, 0][None, None, :] * carry_in[:, :, None]
    backward_factor = jnp.reshape(strength * matrix[0, size - 1], (1, 1))
    unused, carry_next = entering(
        (backward_factor, forward_value[:, :, 0]), "slab", affine_combine, (unit, zero_rows), True
    )
    depth_step = (
        forward_value + strength * matrix[:, size - 1][None, None, :] * carry_next[:, :, None]
    )
    increment = lax.all_to_all(depth_step, "pencil", split_axis=0, concat_axis=1, tiled=True)
    return density + increment


def solution(mesh):
    in_specs = (P("pencil", None, "slab"), P("pencil", None, "slab"), P(), P(), P(), P())
    out_specs = P("pencil", None, "slab")
    return jax.shard_map(
        per_device, mesh=mesh, in_specs=in_specs, out_specs=out_specs, check_vma=False
    )
```

profile of v0, /device:TPU:0, one launch (start us, length us, event | category | flops | bytes accessed | tf_op | source)
XLA Modules:
  0.0 501.9 jit_solution(8275019180080528345)
XLA Ops:
  0.0 11.2 %fusion.34 = (f32[16,768,1]{2,1,0:T(8,128)}, f32[16,768,1]{2,1,0:T(8,128)}) fusion(f32[16,768,128]{2,1,0:T(8,128)} %param.14), kind=kLoop, calls=%fused_computation.71 | loop fusion | bytes 196608 | tf_op jit(solution)/shard_map/slice | solution.py:13
  11.2 4.4 copy.70
  15.6 2.4 collective-permute-start
  18.0 4.4 copy.71
  22.4 1.3 collective-permute-start.1
  23.7 4.0 copy.41
  27.7 3.9 copy.42
  31.7 2.3 pad_maximum_fusion.10
  34.4 1.3 collective-permute-start.2
  36.2 5.3 %collective-permute-start.3 = (f32[1,768,130]{1,0,2:T(1,128)S(1)}, f32[1,768,130]{1,0,2:T(1,128)S(1)}, u32[]{:S(2)}, u32[]{:S(2)}) collective-permute-start(f32[1,768,130]{1,0,2:T(1,128)S(1)} %copy.45), channel_id=1, source_target_pairs={{0,1},{1,2},{2,3},{3,4},{4,5},{5,6},{6,7},{8,9},{9,10},{10,11},{11... | collective-permute-start | bytes 1198088 | tf_op jit(solution)/shard_map/ppermute | solution.py:14
  41.5 0.6 fusion.36
  42.2 4.6 collective-permute-done.2
  47.2 10.4 %collective-permute-done.3 = f32[1,768,130]{1,0,2:T(1,128)S(1)} collective-permute-done((f32[1,768,130]{1,0,2:T(1,128)S(1)}, f32[1,768,130]{1,0,2:T(1,128)S(1)}, u32[]{:S(2)}, u32[]{:S(2)}) %collective-permute-start.3) | collective-permute-done | bytes 399392 | tf_op jit(solution)/shard_map/ppermute | solution.py:14
  58.1 30.9 %fusion.17 = f32[16,768,128]{2,1,0:T(8,128)} fusion(f32[16,768,128]{2,1,0:T(8,128)} %param.15, f32[16,768,128]{2,1,0:T(8,128)} %param.14, f32[16,768,1]{2,1,0:T(8,128)} %copy.41, f32[16,768,1]{2,1,0:T(8,128)} %copy.42, f32[1,768,130]{2,1,0:T(8,128)S(1)} %copy.46, f32[1,768,130]{2,1,0:T(8,128)S(1)} %copy.44, f32[]{:T(128)} %bitcast.16, f32[]{:T(128)} %bitcast.15, ...), kind=kLoop, calls=%fused_computation.35 | loop fusion | flops 34603008 | bytes 19771404 | tf_op jit(solution)/shard_map/add | solution.py:81
  89.0 24.1 %while.70 = (s32[]{:T(128)}, f32[16,6,128,128]{3,2,1,0:T(8,128)}, f32[16,128]{1,0:T(8,128)S(1)}, f32[6,128,128]{2,1,0:T(8,128)S(1)}, f32[16,6,128,128]{3,2,1,0:T(8,128)}, /*index=5*/f32[]{:T(128)}, s32[]{:T(128)}) while((s32[]{:T(128)}, f32[16,6,128,128]{3,2,1,0:T(8,128)}, f32[16,128]{1,0:T(8,128)S(1)}, f32[6,128,128]{2,1,0:T(8,128)S(1)}, ...), condition=%wide.region_1.2_spmd, body=%wide.region_0.1_spmd.sunk | while | flops 403177600 | bytes 3370069 | solution.py:52
  89.1 0.7 fusion.41
  89.8 3.2 bitcast_dynamic-update-slice_fusion.2
  93.1 0.7 fusion.41
  93.8 3.2 bitcast_dynamic-update-slice_fusion.2
  97.1 0.7 fusion.41
  97.8 3.2 bitcast_dynamic-update-slice_fusion.2
  101.1 0.7 fusion.41
  101.9 3.2 bitcast_dynamic-update-slice_fusion.2
  105.2 0.7 fusion.41
  105.9 3.2 bitcast_dynamic-update-slice_fusion.2
  109.2 0.7 fusion.41
  109.9 3.2 bitcast_dynamic-update-slice_fusion.2
  113.2 23.1 %while.71 = (s32[]{:T(128)}, f32[16,6,128,128]{3,2,1,0:T(8,128)}, f32[16,128]{1,0:T(8,128)S(1)}, f32[]{:T(128)}, f32[6,128,128]{2,1,0:T(8,128)S(1)}, /*index=5*/s32[]{:T(128)}, s32[]{:T(128)}, s32[]{:T(128)}, s32[]{:T(128)}) while((s32[]{:T(128)}, f32[16,6,128,128]{3,2,1,0:T(8,128)}, f32[16,128]{1,0:T(8,128)S(1)}, f32[]{:T(128)}, ...), condition=%wide.region_3.4_spmd, body=%wide.region_2.3_spmd.sunk | while | flops 528518 | bytes 5555867 | solution.py:63
  113.3 0.6 fusion.42
  114.0 2.4 constant_dynamic-slice_fusion.13
  117.2 0.6 fusion.42
  117.8 2.4 constant_dynamic-slice_fusion.13
  121.0 0.6 fusion.42
  121.7 2.4 constant_dynamic-slice_fusion.13
  124.9 0.6 fusion.42
  125.5 2.4 constant_dynamic-slice_fusion.13
  128.7 0.6 fusion.42
  129.4 2.4 constant_dynamic-slice_fusion.13
  132.6 0.6 fusion.42
  133.2 2.4 constant_dynamic-slice_fusion.13
  136.3 9.0 %copy.52 = f32[16,6,128,128]{3,0,2,1:T(8,128)} copy(f32[16,6,128,128]{3,2,1,0:T(8,128)} %get-tuple-element.414) | data formatting | bytes 12582912 | tf_op jit(solution)/shard_map/while | solution.py:63
  145.3 5.9 %all-to-all-start = ((f32[16,768,128]{2,0,1:T(8,128)}), f32[16,768,128]{2,0,1:T(8,128)}, u32[]{:S(2)}, u32[]{:S(2)}) async-start(f32[16,768,128]{2,0,1:T(8,128)} %bitcast.110), calls=%async_computation | async-start | bytes 12582912 | tf_op jit(solution)/shard_map/all_to_all | solution.py:85
  154.9 0.8 dynamic-update-slice
  155.6 0.8 dynamic-update-slice.1
  156.4 7.5 %all-reduce.3 = (f32[4]{0:T(128)S(1)}, f32[4]{0:T(128)S(1)}) all-reduce(f32[4]{0:T(128)S(1)} %dynamic-update-slice, f32[4]{0:T(128)S(1)} %dynamic-update-slice.1), channel_id=1, replica_groups=mesh['slab'=4,'pencil'=8] {'slab'}, use_global_device_ids=true, to_apply=%add.1 | all-reduce | flops 8 | bytes 64
  163.8 0.7 fusion.23
  164.6 0.8 fusion.28
  165.4 124.3 %all-to-all-done = f32[16,768,128]{2,0,1:T(8,128)} async-done(((f32[16,768,128]{2,0,1:T(8,128)}), f32[16,768,128]{2,0,1:T(8,128)}, u32[]{:S(2)}, u32[]{:S(2)}) %all-to-all-start) | async-done | bytes 6291488 | tf_op jit(solution)/shard_map/all_to_all | solution.py:85
  289.7 4.7 copy.54
  294.4 13.4 %fusion.9 = f32[12288,128]{1,0:T(8,128)S(1)} fusion(f32[16,8,96,128]{3,2,1,0:T(8,128)S(1)} %bitcast.107, f32[128]{0:T(128)S(1)} %get-tuple-element.498, f32[128]{0:T(128)S(1)} %get-tuple-element.497, f32[1,128,128]{2,1,0:T(8,128)S(1)} %copy-done.3), kind=kOutput, calls=%fused_computation.26 | convolution fusion | flops 2419064832 | bytes 12649472 | tf_op jit(solution)/shard_map/while/body/eval_jaxpr/pkq,jk->pjq/dot_general | solution.py:46
  307.8 6.4 %fusion.29 = f32[128,96,128]{0,2,1:T(8,128)S(1)} fusion(f32[128,96,128]{0,2,1:T(8,128)S(1)} %bitcast.108, f32[4,128,128]{2,1,0:T(8,128)S(1)} %copy-done, s32[]{:T(128)S(6)} %select_n.60), kind=kOutput, calls=%fused_computation.65 | convolution fusion | flops 2415919104 | bytes 12648452 | tf_op jit(solution)/shard_map/yxk,jk->yxj/dot_general | solution.py:92
  314.2 2.7 copy-done.1
  317.0 5.8 %all-gather = f32[512,96,1]{0,2,1:T(1,128)S(1)} all-gather(f32[128,96,1]{0,2,1:T(1,128)S(1)} %slice.140), channel_id=2, replica_groups=mesh['slab'=4,'pencil'=8] {'slab'}, dimensions={0}, use_global_device_ids=true | all-gather | bytes 245760 | tf_op jit(solution)/shard_map/all_gather | solution.py:24
  322.9 3.9 multiply_add_fusion.1
  326.8 10.0 %all-gather.1 = f32[512,96,1]{0,2,1:T(1,128)S(1)} all-gather(f32[128,96,1]{0,2,1:T(1,128)S(1)} %slice.143), channel_id=3, replica_groups=mesh['slab'=4,'pencil'=8] {'slab'}, dimensions={0}, use_global_device_ids=true | all-gather | bytes 245760 | tf_op jit(solution)/shard_map/all_gather | solution.py:24
  336.9 4.3 while.73
  337.6 0.6 bitcast_add_fusion.6
  339.1 0.6 bitcast_add_fusion.6
  340.5 0.6 bitcast_add_fusion.6
  341.3 7.1 %multiply_add_fusion = f32[128,96,128]{0,2,1:T(8,128)} fusion(f32[128,96]{0,1:T(8,128)S(1)} %copy.59, f32[128]{0:T(128)S(1)} %get-tuple-element.495, f32[128,96,128]{0,2,1:T(8,128)} %copy-done.1, f32[128,96]{0,1:T(8,128)S(1)} %copy.57, f32[128]{0:T(128)S(1)} %get-tuple-element.496), kind=kLoop, calls=%fused_computation.50 | loop fusion | flops 6291456 | bytes 12682240 | tf_op jit(solution)/shard_map/add | solution.py:109
  348.4 6.6 %copy.60 = f32[128,96,128]{2,1,0:T(8,128)} copy(f32[128,96,128]{0,2,1:T(8,128)} %multiply_add_fusion) | data formatting | bytes 12582912 | tf_op jit(solution)/shard_map/add | solution.py:109
  355.0 141.7 %all_to_all.33 = f32[128,96,128]{2,1,0:T(8,128)S(1)} all-to-all(f32[128,96,128]{2,1,0:T(8,128)} %copy.60), channel_id=1, replica_groups=mesh['slab'=4,'pencil'=8] {'pencil'}, dimensions={0} | all-to-all | bytes 12582912 | tf_op jit(solution)/shard_map/all_to_all | solution.py:111
  497.3 1.0 slice-done.1
  498.3 3.4 bitcast_add_fusion.2
  (88 shorter events, 10.9 us)
Async XLA Ops:
  0.0 151.2 %copy-start = (f32[4,128,128]{2,1,0:T(8,128)S(1)}, f32[4,128,128]{2,1,0:T(8,128)}, u32[]{:S(2)}) copy-start(f32[4,128,128]{2,1,0:T(8,128)} %param.19) | copy-start | bytes 786436
  15.6 8.1 %collective-permute-start = (f32[16,768,1]{1,0,2:T(8,128)S(1)}, f32[16,768,1]{1,0,2:T(8,128)S(1)}, u32[]{:S(2)}, u32[]{:S(2)}) collective-permute-start(f32[16,768,1]{1,0,2:T(8,128)S(1)} %copy.70), channel_id=1, source_target_pairs={{0,8},{8,16},{16,24},{1,9},{9,17},{17,25},{2,10},{10,18},{18,26},{... | collective-permute-start | bytes 147464 | tf_op jit(solution)/shard_map/ppermute | solution.py:14
  22.4 5.3 %collective-permute-start.1 = (f32[16,768,1]{1,0,2:T(8,128)S(1)}, f32[16,768,1]{1,0,2:T(8,128)S(1)}, u32[]{:S(2)}, u32[]{:S(2)}) collective-permute-start(f32[16,768,1]{1,0,2:T(8,128)S(1)} %copy.71), channel_id=1, source_target_pairs={{8,0},{16,8},{24,16},{9,1},{17,9},{25,17},{10,2},{18,10},{26,18},{... | collective-permute-start | bytes 147464 | tf_op jit(solution)/shard_map/ppermute | solution.py:15
  31.7 9.8 %copy-start.4 = (f32[3]{0:T(128)S(1)}, f32[3]{0:T(128)}, u32[]{:S(2)}) copy-start(f32[3]{0:T(128)} %param.16) | copy-start | bytes 40
  34.4 12.3 %collective-permute-start.2 = (f32[1,768,130]{1,0,2:T(1,128)S(1)}, f32[1,768,130]{1,0,2:T(1,128)S(1)}, u32[]{:S(2)}, u32[]{:S(2)}) collective-permute-start(f32[1,768,130]{1,0,2:T(1,128)S(1)} %copy.43), channel_id=1, source_target_pairs={{1,0},{2,1},{3,2},{4,3},{5,4},{6,5},{7,6},{9,8},{10,9},{11,10},{12... | collective-permute-start | bytes 1198088 | tf_op jit(solution)/shard_map/ppermute | solution.py:15
  36.2 21.4 %collective-permute-start.3 = (f32[1,768,130]{1,0,2:T(1,128)S(1)}, f32[1,768,130]{1,0,2:T(1,128)S(1)}, u32[]{:S(2)}, u32[]{:S(2)}) collective-permute-start(f32[1,768,130]{1,0,2:T(1,128)S(1)} %copy.45), channel_id=1, source_target_pairs={{0,1},{1,2},{2,3},{3,4},{4,5},{5,6},{6,7},{8,9},{9,10},{10,11},{11... | collective-permute-start | bytes 1198088 | tf_op jit(solution)/shard_map/ppermute | solution.py:14
  58.1 30.9 %copy-start.2 = (f32[6,128,128]{2,1,0:T(8,128)S(1)}, f32[6,128,128]{2,1,0:T(8,128)}, u32[]{:S(2)}) copy-start(f32[6,128,128]{2,1,0:T(8,128)} %param.17) | copy-start | bytes 1179652
  145.3 9.0 %copy-start.5 = (u32[32]{0:T(128)S(1)}, u32[32]{0:T(128)}, u32[]{:S(2)}) copy-start(u32[32]{0:T(128)} %constant.197) | copy-start | bytes 388
  145.3 19.3 %copy-start.3 = (f32[1,128,128]{2,1,0:T(8,128)S(1)}, f32[1,128,128]{2,1,0:T(8,128)}, u32[]{:S(2)}) copy-start(f32[1,128,128]{2,1,0:T(8,128)} %param.18) | copy-start | bytes 196612
  145.3 144.4 %all-to-all-start = ((f32[16,768,128]{2,0,1:T(8,128)}), f32[16,768,128]{2,0,1:T(8,128)}, u32[]{:S(2)}, u32[]{:S(2)}) async-start(f32[16,768,128]{2,0,1:T(8,128)} %bitcast.110), calls=%async_computation | async-start | bytes 12582912 | tf_op jit(solution)/shard_map/all_to_all | solution.py:85
  314.2 2.7 copy-start.1
  355.0 142.4 %slice-start = ((s8[6291456]{0:T(1024)(128)(4,1)}), s8[4194304]{0:T(1024)(128)(4,1)S(1)}, s32[]{:S(2)}) async-start(s8[6291456]{0:T(1024)(128)(4,1)} %bitcast.105), calls=%async_computation.2 | async-start | bytes 8388608
  496.7 1.6 slice-start.1
where the time goes:
time: 507 us; the launch traced here: 502 us
  blocking collectives  165 us (33%)
  waiting for transfers between devices  139 us (27%)
  other arithmetic  73.9 us (15%)
  local copies, waits for them, and re-layouts  64.7 us (13%)
  matrix products  39.3 us (8%)
  starting transfers between devices  16.2 us (3%)
    all_to_all x1, blocking collectives, per_device(): lax.all_to_all(depth_step, 'pencil', split_axis=0, concat_axis=1, tiled=T...  142 us
    all_to_all x1, waiting for transfers between devices, per_device(): lax.all_to_all(width_step, 'pencil', split_axis=1, concat_axis=0, tiled=T...  124 us
    dot_general x7, matrix products, forward(): jnp.einsum('pkq,jk->pjq', piece, matrix, precision=lax.Precision.HIGHEST)  32.9 us
    add x1, other arithmetic, per_device(): 2.0 * (coupling[0] * along_width + coupling[1] * along_height + coupling[...  30.9 us
    all_gather x2, blocking collectives, entering(): gathered = jax.tree.map(lambda a: lax.all_gather(a, axis), part)  15.8 us
    unnamed x23, local copies, waits for them, and re-layouts  14.6 us
    dynamic_slice x6, other arithmetic, backward(): value = lax.dynamic_index_in_dim(result, current, 1, keepdims=False)  14.4 us
    slice x2, local copies, waits for them, and re-layouts, extended(): leading = lax.slice_in_dim(value, 0, width, axis=dim)  11.6 us
  transfers between devices with their start and end apart: 5, of which 3 were waited for; matrix products, arithmetic and copies ran while one was open for 3% of the time, Pallas kernels for 0%

commit v1 on v0

--- a/solution.py
+++ b/solution.py
@@ -2,6 +2,18 @@
 import jax.numpy as jnp
 from jax import lax
 from jax.sharding import PartitionSpec as P
+
+
+def split_up(x, dim, size):
+    lengths = x.shape
+    pieces = x.reshape(*lengths[:dim], size, lengths[dim] // size, *lengths[dim + 1 :])
+    return jnp.moveaxis(pieces, dim, 0)
+
+
+def laid_out(pieces, dim):
+    pieces = jnp.moveaxis(pieces, 0, dim)
+    shape = pieces.shape
+    return pieces.reshape(*shape[:dim], shape[dim] * shape[dim + 1], *shape[dim + 2 :])
 
 
 def extended(value, sides, width):
@@ -108,7 +120,14 @@
     depth_step = (
         forward_value + strength * matrix[:, size - 1][None, None, :] * carry_next[:, :, None]
     )
-    increment = lax.all_to_all(depth_step, "pencil", split_axis=0, concat_axis=1, tiled=True)
+    length_2, place_2 = (lax.axis_size("pencil"), lax.axis_index("pencil"))
+    tiles = split_up(depth_step, 0, length_2)
+    outs = [tiles[place_2]]
+    for hop in range(1, length_2):
+        sent = tiles[place_2 ^ hop]
+        outs.append(lax.ppermute(sent, "pencil", [(i_2, i_2 ^ hop) for i_2 in range(length_2)]))
+    tiles = jnp.stack(outs)[place_2 ^ jnp.arange(length_2)]
+    increment = laid_out(tiles, 1)
     return density + increment
 
 

time: 507 us -> 519 us (1.024)
  the two profiles are of different devices: /device:TPU:0 before, /device:TPU:8 now
where the time goes in v1:
time: 519 us; the launch traced here: 514 us
  waiting for transfers between devices  263 us (51%)
  local copies, waits for them, and re-layouts  84.5 us (16%)
  other arithmetic  74.1 us (14%)
  matrix products  39.3 us (8%)
  starting transfers between devices  25.7 us (5%)
  blocking collectives  23.3 us (4%)
    ppermute x7, waiting for transfers between devices, per_device(): lax.ppermute(sent, 'pencil', [(i_2, i_2 ^ hop) for i_2 in range(length_2)])  127 us
    all_to_all x1, waiting for transfers between devices, per_device(): lax.all_to_all(width_step, 'pencil', split_axis=1, concat_axis=0, tiled=T...  122 us
    dot_general x7, matrix products, forward(): jnp.einsum('pkq,jk->pjq', piece, matrix, precision=lax.Precision.HIGHEST)  32.9 us
    add x1, other arithmetic, per_device(): 2.0 * (coupling[0] * along_width + coupling[1] * along_height + coupling[...  30.9 us
    unnamed x29, local copies, waits for them, and re-layouts  19.8 us
    all_gather x2, blocking collectives, entering(): gathered = jax.tree.map(lambda a: lax.all_gather(a, axis), part)  16.1 us
    dynamic_slice x6, other arithmetic, backward(): value = lax.dynamic_index_in_dim(result, current, 1, keepdims=False)  14.4 us
    ppermute x2, waiting for transfers between devices, extended(): after = lax.ppermute(leading, axis, down)  13.6 us
  transfers between devices with their start and end apart: 12, of which 9 were waited for; matrix products, arithmetic and copies ran while one was open for 4% of the time, Pallas kernels for 0%

profile of v1, /device:TPU:8, one launch (start us, length us, event | category | flops | bytes accessed | tf_op | source)
XLA Modules:
  0.0 513.6 jit_solution(18121074439105657277)
XLA Ops:
  0.0 11.2 %fusion.35 = (f32[16,768,1]{2,1,0:T(8,128)}, f32[16,768,1]{2,1,0:T(8,128)}) fusion(f32[16,768,128]{2,1,0:T(8,128)} %param.14), kind=kLoop, calls=%fused_computation.90 | loop fusion | bytes 196608 | tf_op jit(solution)/shard_map/slice | solution.py:25
  11.2 4.4 copy.70
  15.6 1.7 collective-permute-start
  17.3 4.4 copy.71
  21.8 1.3 collective-permute-start.1
  23.1 4.0 copy.41
  27.1 3.9 copy.42
  31.0 2.3 pad_maximum_fusion.10
  33.7 3.3 collective-permute-start.2
  37.5 3.1 collective-permute-start.3
  41.3 13.6 %collective-permute-done.2 = f32[1,768,130]{1,0,2:T(1,128)S(1)} collective-permute-done((f32[1,768,130]{1,0,2:T(1,128)S(1)}, f32[1,768,130]{1,0,2:T(1,128)S(1)}, u32[]{:S(2)}, u32[]{:S(2)}) %collective-permute-start.2) | collective-permute-done | bytes 399392 | tf_op jit(solution)/shard_map/ppermute | solution.py:27
  55.3 0.8 collective-permute-done.3
  56.6 30.9 %fusion.17 = f32[16,768,128]{2,1,0:T(8,128)} fusion(f32[16,768,128]{2,1,0:T(8,128)} %param.15, f32[16,768,128]{2,1,0:T(8,128)} %param.14, f32[16,768,1]{2,1,0:T(8,128)} %copy.41, f32[16,768,1]{2,1,0:T(8,128)} %copy.42, f32[1,768,130]{2,1,0:T(8,128)S(1)} %copy.46, f32[1,768,130]{2,1,0:T(8,128)S(1)} %copy.44, f32[]{:T(128)} %bitcast.16, f32[]{:T(128)} %bitcast.15, ...), kind=kLoop, calls=%fused_computation.36 | loop fusion | flops 34603008 | bytes 19771404 | tf_op jit(solution)/shard_map/add | solution.py:93
  87.5 24.2 %while.70 = (s32[]{:T(128)}, f32[16,6,128,128]{3,2,1,0:T(8,128)}, f32[16,128]{1,0:T(8,128)S(1)}, f32[6,128,128]{2,1,0:T(8,128)S(1)}, f32[16,6,128,128]{3,2,1,0:T(8,128)}, /*index=5*/f32[]{:T(128)}, s32[]{:T(128)}) while((s32[]{:T(128)}, f32[16,6,128,128]{3,2,1,0:T(8,128)}, f32[16,128]{1,0:T(8,128)S(1)}, f32[6,128,128]{2,1,0:T(8,128)S(1)}, ...), condition=%wide.region_1.2_spmd, body=%wide.region_0.1_spmd.sunk | while | flops 403177600 | bytes 3370069 | solution.py:64
  88.3 3.2 bitcast_dynamic-update-slice_fusion.9
  92.3 3.2 bitcast_dynamic-update-slice_fusion.9
  96.4 3.2 bitcast_dynamic-update-slice_fusion.9
  100.4 3.2 bitcast_dynamic-update-slice_fusion.9
  104.4 3.2 bitcast_dynamic-update-slice_fusion.9
  108.5 3.2 bitcast_dynamic-update-slice_fusion.9
  111.7 23.2 %while.71 = (s32[]{:T(128)}, f32[16,6,128,128]{3,2,1,0:T(8,128)}, f32[16,128]{1,0:T(8,128)S(1)}, f32[]{:T(128)}, f32[6,128,128]{2,1,0:T(8,128)S(1)}, /*index=5*/s32[]{:T(128)}, s32[]{:T(128)}, s32[]{:T(128)}, s32[]{:T(128)}) while((s32[]{:T(128)}, f32[16,6,128,128]{3,2,1,0:T(8,128)}, f32[16,128]{1,0:T(8,128)S(1)}, f32[]{:T(128)}, ...), condition=%wide.region_3.4_spmd, body=%wide.region_2.3_spmd.sunk | while | flops 528518 | bytes 5555867 | solution.py:75
  112.5 2.4 constant_dynamic-slice_fusion.13
  116.4 2.4 constant_dynamic-slice_fusion.13
  120.3 2.4 constant_dynamic-slice_fusion.13
  124.1 2.4 constant_dynamic-slice_fusion.13
  128.0 2.4 constant_dynamic-slice_fusion.13
  131.8 2.4 constant_dynamic-slice_fusion.13
  134.9 9.0 %copy.52 = f32[16,6,128,128]{3,0,2,1:T(8,128)} copy(f32[16,6,128,128]{3,2,1,0:T(8,128)} %get-tuple-element.414) | data formatting | bytes 12582912 | tf_op jit(solution)/shard_map/while | solution.py:75
  143.9 6.4 %all-to-all-start = ((f32[16,768,128]{2,0,1:T(8,128)}), f32[16,768,128]{2,0,1:T(8,128)}, u32[]{:S(2)}, u32[]{:S(2)}) async-start(f32[16,768,128]{2,0,1:T(8,128)} %bitcast.139), calls=%async_computation | async-start | bytes 12582912 | tf_op jit(solution)/shard_map/all_to_all | solution.py:97
  154.6 0.8 dynamic-update-slice.1
  155.4 7.2 %all-reduce.3 = (f32[4]{0:T(128)S(1)}, f32[4]{0:T(128)S(1)}) all-reduce(f32[4]{0:T(128)S(1)} %dynamic-update-slice, f32[4]{0:T(128)S(1)} %dynamic-update-slice.1), channel_id=1, replica_groups=mesh['slab'=4,'pencil'=8] {'slab'}, use_global_device_ids=true, to_apply=%add.1 | all-reduce | flops 8 | bytes 64
  163.3 0.9 fusion.28
  164.2 122.0 %all-to-all-done = f32[16,768,128]{2,0,1:T(8,128)} async-done(((f32[16,768,128]{2,0,1:T(8,128)}), f32[16,768,128]{2,0,1:T(8,128)}, u32[]{:S(2)}, u32[]{:S(2)}) %all-to-all-start) | async-done | bytes 6291488 | tf_op jit(solution)/shard_map/all_to_all | solution.py:97
  286.2 4.7 copy.54
  290.9 13.4 %fusion.9 = f32[12288,128]{1,0:T(8,128)S(1)} fusion(f32[16,8,96,128]{3,2,1,0:T(8,128)S(1)} %bitcast.136, f32[128]{0:T(128)S(1)} %get-tuple-element.498, f32[128]{0:T(128)S(1)} %get-tuple-element.497, f32[1,128,128]{2,1,0:T(8,128)S(1)} %copy-done.3), kind=kOutput, calls=%fused_computation.27 | convolution fusion | flops 2419064832 | bytes 12649472 | tf_op jit(solution)/shard_map/while/body/eval_jaxpr/pkq,jk->pjq/dot_general | solution.py:58
  304.3 6.4 %fusion.29 = f32[128,96,128]{0,2,1:T(8,128)S(1)} fusion(f32[128,96,128]{0,2,1:T(8,128)S(1)} %bitcast.137, f32[4,128,128]{2,1,0:T(8,128)S(1)} %copy-done, s32[]{:T(128)S(6)} %select_n.94), kind=kOutput, calls=%fused_computation.81 | convolution fusion | flops 2415919104 | bytes 12648452 | tf_op jit(solution)/shard_map/yxk,jk->yxj/dot_general | solution.py:104
  310.7 2.7 copy-done.1
  313.5 5.8 %all-gather = f32[512,96,1]{0,2,1:T(1,128)S(1)} all-gather(f32[128,96,1]{0,2,1:T(1,128)S(1)} %slice.142), channel_id=2, replica_groups=mesh['slab'=4,'pencil'=8] {'slab'}, dimensions={0}, use_global_device_ids=true | all-gather | bytes 245760 | tf_op jit(solution)/shard_map/all_gather | solution.py:36
  319.3 3.9 multiply_add_fusion.1
  323.3 10.3 %all-gather.1 = f32[512,96,1]{0,2,1:T(1,128)S(1)} all-gather(f32[128,96,1]{0,2,1:T(1,128)S(1)} %slice.145), channel_id=3, replica_groups=mesh['slab'=4,'pencil'=8] {'slab'}, dimensions={0}, use_global_device_ids=true | all-gather | bytes 245760 | tf_op jit(solution)/shard_map/all_gather | solution.py:36
  333.6 4.1 while.73
  337.8 7.1 %multiply_add_fusion = f32[128,96,128]{0,2,1:T(8,128)} fusion(f32[128,96]{0,1:T(8,128)S(1)} %copy.59, f32[128]{0:T(128)S(1)} %get-tuple-element.495, f32[128,96,128]{0,2,1:T(8,128)} %copy-done.1, f32[128,96]{0,1:T(8,128)S(1)} %copy.57, f32[128]{0:T(128)S(1)} %get-tuple-element.496), kind=kLoop, calls=%fused_computation.51 | loop fusion | flops 6291456 | bytes 12682240 | tf_op jit(solution)/shard_map/add | solution.py:121
  344.8 7.0 %copy.60 = f32[128,96,128]{2,1,0:T(8,128)} copy(f32[128,96,128]{0,2,1:T(8,128)} %multiply_add_fusion) | data formatting | bytes 12582912 | tf_op jit(solution)/shard_map/add | solution.py:121
  351.8 4.1 dynamic-slice_bitcast_fusion.1
  356.6 3.5 collective-permute-start.5
  360.1 2.8 collective-permute-start.7
  362.9 1.1 collective-permute-start.8
  363.9 10.4 %collective-permute-done.4 = f32[16,96,128]{2,1,0:T(8,128)S(1)} collective-permute-done((f32[16,96,128]{2,1,0:T(8,128)S(1)}, f32[16,96,128]{2,1,0:T(8,128)S(1)}, u32[]{:S(2)}, u32[]{:S(2)}) %collective-permute-start.4) | collective-permute-done | bytes 786464 | tf_op jit(solution)/shard_map/ppermute | solution.py:128
  375.0 0.9 bitcast_dynamic-update-slice_fusion.7
  375.9 33.0 %collective-permute-done.5 = f32[16,96,128]{2,1,0:T(8,128)S(1)} collective-permute-done((f32[16,96,128]{2,1,0:T(8,128)S(1)}, f32[16,96,128]{2,1,0:T(8,128)S(1)}, u32[]{:S(2)}, u32[]{:S(2)}) %collective-permute-start.5) | collective-permute-done | bytes 786464 | tf_op jit(solution)/shard_map/ppermute | solution.py:128
  408.9 1.3 collective-permute-start.10
  410.2 0.9 bitcast_dynamic-update-slice_fusion.6
  411.2 12.4 %collective-permute-done.6 = f32[16,96,128]{2,1,0:T(8,128)S(1)} collective-permute-done((f32[16,96,128]{2,1,0:T(8,128)S(1)}, f32[16,96,128]{2,1,0:T(8,128)S(1)}, u32[]{:S(2)}, u32[]{:S(2)}) %collective-permute-start.6) | collective-permute-done | bytes 786464 | tf_op jit(solution)/shard_map/ppermute | solution.py:128
  423.5 0.9 bitcast_dynamic-update-slice_fusion.5
  424.5 0.9 bitcast_dynamic-update-slice_fusion.4
  425.4 39.6 %collective-permute-done.8 = f32[16,96,128]{2,1,0:T(8,128)S(1)} collective-permute-done((f32[16,96,128]{2,1,0:T(8,128)S(1)}, f32[16,96,128]{2,1,0:T(8,128)S(1)}, u32[]{:S(2)}, u32[]{:S(2)}) %collective-permute-start.8) | collective-permute-done | bytes 786464 | tf_op jit(solution)/shard_map/ppermute | solution.py:128
  465.1 0.9 bitcast_dynamic-update-slice_fusion.3
  466.0 17.0 %collective-permute-done.9 = f32[16,96,128]{2,1,0:T(8,128)S(1)} collective-permute-done((f32[16,96,128]{2,1,0:T(8,128)S(1)}, f32[16,96,128]{2,1,0:T(8,128)S(1)}, u32[]{:S(2)}, u32[]{:S(2)}) %collective-permute-start.9) | collective-permute-done | bytes 786464 | tf_op jit(solution)/shard_map/ppermute | solution.py:128
  483.0 0.9 bitcast_dynamic-update-slice_fusion.2
  483.9 14.1 %collective-permute-done.10 = f32[16,96,128]{2,1,0:T(8,128)S(1)} collective-permute-done((f32[16,96,128]{2,1,0:T(8,128)S(1)}, f32[16,96,128]{2,1,0:T(8,128)S(1)}, u32[]{:S(2)}, u32[]{:S(2)}) %collective-permute-start.10) | collective-permute-done | bytes 786464 | tf_op jit(solution)/shard_map/ppermute | solution.py:128
  498.1 0.9 bitcast_dynamic-update-slice_fusion.1
  499.0 6.6 %gather_fusion = f32[8,16,96,128]{3,2,1,0:T(8,128)} fusion(f32[8,16,96,128]{3,2,1,0:T(8,128)} %bitcast_dynamic-update-slice_fusion.1, s32[1024]{0:T(1024)S(1)} %pad_clamp_fusion), kind=kCustom, calls=%fused_computation | custom fusion | bytes 12582944 | tf_op jit(solution)/shard_map/gather | solution.py:129
  505.6 3.4 copy.61
  509.6 3.7 bitcast_add_fusion.2
  (112 shorter events, 24.3 us)
Async XLA Ops:
  0.0 150.3 %copy-start = (f32[4,128,128]{2,1,0:T(8,128)S(1)}, f32[4,128,128]{2,1,0:T(8,128)}, u32[]{:S(2)}) copy-start(f32[4,128,128]{2,1,0:T(8,128)} %param.19) | copy-start | bytes 786436
  15.6 7.5 %collective-permute-start = (f32[16,768,1]{1,0,2:T(8,128)S(1)}, f32[16,768,1]{1,0,2:T(8,128)S(1)}, u32[]{:S(2)}, u32[]{:S(2)}) collective-permute-start(f32[16,768,1]{1,0,2:T(8,128)S(1)} %copy.70), channel_id=1, source_target_pairs={{0,8},{8,16},{16,24},{1,9},{9,17},{17,25},{2,10},{10,18},{18,26},{... | collective-permute-start | bytes 147464 | tf_op jit(solution)/shard_map/ppermute | solution.py:26
  21.8 5.3 %collective-permute-start.1 = (f32[16,768,1]{1,0,2:T(8,128)S(1)}, f32[16,768,1]{1,0,2:T(8,128)S(1)}, u32[]{:S(2)}, u32[]{:S(2)}) collective-permute-start(f32[16,768,1]{1,0,2:T(8,128)S(1)} %copy.71), channel_id=1, source_target_pairs={{8,0},{16,8},{24,16},{9,1},{17,9},{25,17},{10,2},{18,10},{26,18},{... | collective-permute-start | bytes 147464 | tf_op jit(solution)/shard_map/ppermute | solution.py:27
  31.0 9.6 %copy-start.4 = (f32[3]{0:T(128)S(1)}, f32[3]{0:T(128)}, u32[]{:S(2)}) copy-start(f32[3]{0:T(128)} %param.16) | copy-start | bytes 40
  33.7 21.1 %collective-permute-start.2 = (f32[1,768,130]{1,0,2:T(1,128)S(1)}, f32[1,768,130]{1,0,2:T(1,128)S(1)}, u32[]{:S(2)}, u32[]{:S(2)}) collective-permute-start(f32[1,768,130]{1,0,2:T(1,128)S(1)} %copy.43), channel_id=1, source_target_pairs={{1,0},{2,1},{3,2},{4,3},{5,4},{6,5},{7,6},{9,8},{10,9},{11,10},{12... | collective-permute-start | bytes 1198088 | tf_op jit(solution)/shard_map/ppermute | solution.py:27
  37.5 18.6 %collective-permute-start.3 = (f32[1,768,130]{1,0,2:T(1,128)S(1)}, f32[1,768,130]{1,0,2:T(1,128)S(1)}, u32[]{:S(2)}, u32[]{:S(2)}) collective-permute-start(f32[1,768,130]{1,0,2:T(1,128)S(1)} %copy.45), channel_id=1, source_target_pairs={{0,1},{1,2},{2,3},{3,4},{4,5},{5,6},{6,7},{8,9},{9,10},{10,11},{11... | collective-permute-start | bytes 1198088 | tf_op jit(solution)/shard_map/ppermute | solution.py:26
  56.6 30.9 %copy-start.2 = (f32[6,128,128]{2,1,0:T(8,128)S(1)}, f32[6,128,128]{2,1,0:T(8,128)}, u32[]{:S(2)}) copy-start(f32[6,128,128]{2,1,0:T(8,128)} %param.17) | copy-start | bytes 1179652
  143.9 9.4 %copy-start.5 = (u32[32]{0:T(128)S(1)}, u32[32]{0:T(128)}, u32[]{:S(2)}) copy-start(u32[32]{0:T(128)} %constant.215) | copy-start | bytes 388
  143.9 19.4 %copy-start.3 = (f32[1,128,128]{2,1,0:T(8,128)S(1)}, f32[1,128,128]{2,1,0:T(8,128)}, u32[]{:S(2)}) copy-start(f32[1,128,128]{2,1,0:T(8,128)} %param.18) | copy-start | bytes 196612
  143.9 142.3 %all-to-all-start = ((f32[16,768,128]{2,0,1:T(8,128)}), f32[16,768,128]{2,0,1:T(8,128)}, u32[]{:S(2)}, u32[]{:S(2)}) async-start(f32[16,768,128]{2,0,1:T(8,128)} %bitcast.139), calls=%async_computation | async-start | bytes 12582912 | tf_op jit(solution)/shard_map/all_to_all | solution.py:97
  310.7 2.7 copy-start.1
  355.9 18.4 %collective-permute-start.4 = (f32[16,96,128]{2,1,0:T(8,128)S(1)}, f32[16,96,128]{2,1,0:T(8,128)S(1)}, u32[]{:S(2)}, u32[]{:S(2)}) collective-permute-start(f32[16,96,128]{2,1,0:T(8,128)S(1)} %get-tuple-element.555), channel_id=1, source_target_pairs={{0,1},{1,0},{2,3},{3,2},{4,5},{5,4},{6,7},{7,6},{8,9},{9,8},{10,11... | collective-permute-start | bytes 2359304 | tf_op jit(solution)/shard_map/ppermute | solution.py:128
  356.6 52.4 %collective-permute-start.5 = (f32[16,96,128]{2,1,0:T(8,128)S(1)}, f32[16,96,128]{2,1,0:T(8,128)S(1)}, u32[]{:S(2)}, u32[]{:S(2)}) collective-permute-start(f32[16,96,128]{2,1,0:T(8,128)S(1)} %get-tuple-element.554), channel_id=1, source_target_pairs={{0,2},{1,3},{2,0},{3,1},{4,6},{5,7},{6,4},{7,5},{8,10},{9,11},{10,... | collective-permute-start | bytes 2359304 | tf_op jit(solution)/shard_map/ppermute | solution.py:128
  360.0 63.5 %collective-permute-start.6 = (f32[16,96,128]{2,1,0:T(8,128)S(1)}, f32[16,96,128]{2,1,0:T(8,128)S(1)}, u32[]{:S(2)}, u32[]{:S(2)}) collective-permute-start(f32[16,96,128]{2,1,0:T(8,128)S(1)} %get-tuple-element.553), channel_id=1, source_target_pairs={{0,3},{1,2},{2,1},{3,0},{4,7},{5,6},{6,5},{7,4},{8,11},{9,10},{10,... | collective-permute-start | bytes 2359304 | tf_op jit(solution)/shard_map/ppermute | solution.py:128
  360.1 64.4 %collective-permute-start.7 = (f32[16,96,128]{2,1,0:T(8,128)S(1)}, f32[16,96,128]{2,1,0:T(8,128)S(1)}, u32[]{:S(2)}, u32[]{:S(2)}) collective-permute-start(f32[16,96,128]{2,1,0:T(8,128)S(1)} %get-tuple-element.552), channel_id=1, source_target_pairs={{0,4},{1,5},{2,6},{3,7},{4,0},{5,1},{6,2},{7,3},{8,12},{9,13},{10,... | collective-permute-start | bytes 2359304 | tf_op jit(solution)/shard_map/ppermute | solution.py:128
  362.9 102.2 %collective-permute-start.8 = (f32[16,96,128]{2,1,0:T(8,128)S(1)}, f32[16,96,128]{2,1,0:T(8,128)S(1)}, u32[]{:S(2)}, u32[]{:S(2)}) collective-permute-start(f32[16,96,128]{2,1,0:T(8,128)S(1)} %get-tuple-element.551), channel_id=1, source_target_pairs={{0,5},{1,4},{2,7},{3,6},{4,1},{5,0},{6,3},{7,2},{8,13},{9,12},{10,... | collective-permute-start | bytes 2359304 | tf_op jit(solution)/shard_map/ppermute | solution.py:128
  374.3 108.7 %collective-permute-start.9 = (f32[16,96,128]{2,1,0:T(8,128)S(1)}, f32[16,96,128]{2,1,0:T(8,128)S(1)}, u32[]{:S(2)}, u32[]{:S(2)}) collective-permute-start(f32[16,96,128]{2,1,0:T(8,128)S(1)} %get-tuple-element.550), channel_id=1, source_target_pairs={{0,6},{1,7},{2,4},{3,5},{4,2},{5,3},{6,0},{7,1},{8,14},{9,15},{10,... | collective-permute-start | bytes 2359304 | tf_op jit(solution)/shard_map/ppermute | solution.py:128
  408.9 89.1 %collective-permute-start.10 = (f32[16,96,128]{2,1,0:T(8,128)S(1)}, f32[16,96,128]{2,1,0:T(8,128)S(1)}, u32[]{:S(2)}, u32[]{:S(2)}) collective-permute-start(f32[16,96,128]{2,1,0:T(8,128)S(1)} %get-tuple-element.549), channel_id=1, source_target_pairs={{0,7},{1,6},{2,5},{3,4},{4,3},{5,2},{6,1},{7,0},{8,15},{9,14},{10,... | collective-permute-start | bytes 2359304 | tf_op jit(solution)/shard_map/ppermute | solution.py:128
  499.0 10.0 %slice-start = ((s8[6291456]{0:T(1024)(128)(4,1)}), s8[2097152]{0:T(1024)(128)(4,1)S(1)}, s32[]{:S(2)}) async-start(s8[6291456]{0:T(1024)(128)(4,1)} %bitcast.134), calls=%async_computation.1 | async-start | bytes 4194304
  505.6 4.0 slice-start.1
